TPU v7x, 32 devices: a whole 2x2x4 slice. The times are simulated.
32 devices in a mesh: row: 8 (over z, x), col: 2 (over core), dp: 2 (over y).
Axes of the slice: x: 2, y: 2, z: 4, core: 2. Of those that a mesh axis runs over, the one named last changes fastest.
Arguments:
- pixels: bfloat16 [2, 3, 256, 256], P('dp', None, 'row', 'col'), may hold values from -6 to 6
- cotangent: bfloat16 [2, 64, 64, 1024], P('dp', 'row', 'col'), may hold values from -6 to 6
- embed_weight: bfloat16 [48, 1024], replicated, may hold values from -0.875 to 0.875
- embed_bias: float32 [1024], replicated, may hold values from -4 to 4
- layer_norm_gain: float32 [1024], replicated, may hold values from 0.5 to 1.5
- qkv_weight: bfloat16 [1024, 2304], P('row', ('col', 'dp')), may hold values from -0.1875 to 0.1875
- out_weight: bfloat16 [768, 1024], P('row', ('col', 'dp')), may hold values from -0.21875 to 0.21875
- bias_table: float32 [12, 225], replicated, may hold values from -4 to 404
- rel_index: int32 [64, 64], replicated, may hold values from 0 to 224
- shifts: int32 [2, 2], P('dp'), may hold values from 1 to 7
Outputs:
- out_weight_grad: float32 [768, 1024], P('row', ('col', 'dp'))
- embed_weight_grad: float32 [48, 1024], replicated
- embed_bias_grad: float32 [1024], replicated
- norm_gain_grad: float32 [1024], replicated
- bias_table_grad: float32 [12, 225], replicated
Inputs may be any that keep to these rules, and one draw needn't show every extreme that they name: `rel_index`: each entry names one of the 225 columns of bias_table.
All inputs are finite; a program needn't handle non-finite values.
Results may differ from a plain program's by a relative error of at most 0.023.
Values may be sent and summed in bfloat16 or wider, within the bound.
A program may use at most 64 MiB of HBM per device.

v0:
```python
import jax
import jax.numpy as jnp
from jax import lax
from jax.sharding import PartitionSpec as P

WIN = 8
PATCH = 4
norm_epsilon = 1e-05


def from_behind(value, axis, steps):
    count = lax.axis_size(axis)
    pairs = [(source, (source + steps) % count) for source in range(count)]
    return lax.ppermute(value, axis, pairs)


def make_patches(pixel_block):
    images, channels, pixel_rows, pixel_cols = pixel_block.shape
    grid_rows = pixel_rows // PATCH
    grid_cols = pixel_cols // PATCH
    shaped = pixel_block.reshape(images, channels, grid_rows, PATCH, grid_cols, PATCH)
    return shaped.transpose(0, 2, 4, 1, 3, 5).reshape(
        images, grid_rows, grid_cols, channels * PATCH * PATCH
    )


def embed_cells(patches, embed_weight, embed_bias):
    return (jnp.dot(patches, embed_weight, preferred_element_type=jnp.float32) + embed_bias).astype(
        jnp.bfloat16
    )


def window_split(block):
    rows_all, cols_all, features = block.shape
    shaped = block.reshape(rows_all // WIN, WIN, cols_all // WIN, WIN, features)
    return shaped.transpose(0, 2, 1, 3, 4).reshape(-1, WIN * WIN, features)


def window_join(windows, rows_all, cols_all):
    features = windows.shape[-1]
    shaped = windows.reshape(rows_all // WIN, cols_all // WIN, WIN, WIN, features)
    return shaped.transpose(0, 2, 1, 3, 4).reshape(rows_all, cols_all, features)


def splice_after(own_block, borrowed, offsets, along_dim):
    length = own_block.shape[along_dim]

    def single(own_item, borrowed_item, offset):
        joined = jnp.concatenate([own_item, borrowed_item], along_dim - 1)
        return lax.dynamic_slice_in_dim(joined, offset, length, along_dim - 1)

    return jax.vmap(single)(own_block, borrowed, offsets)


def splice_before(own_block, borrowed, offsets, along_dim):
    length = own_block.shape[along_dim]
    margin = borrowed.shape[along_dim]

    def single(own_item, borrowed_item, offset):
        joined = jnp.concatenate([borrowed_item, own_item], along_dim - 1)
        return lax.dynamic_slice_in_dim(joined, margin - offset, length, along_dim - 1)

    return jax.vmap(single)(own_block, borrowed, offsets)


def attend_forward(cell_windows, labels, layer_norm_gain, qkv_full, bias_full):
    window_count, cell_count, features = cell_windows.shape
    head_count = bias_full.shape[0]
    inner_width = qkv_full.shape[1] // 3
    head_size = inner_width // head_count
    score_scale = head_size ** (-0.5)
    flat_rows = cell_windows.reshape(-1, features).astype(jnp.float32)
    average = jnp.mean(flat_rows, axis=-1, keepdims=True)
    centered_input = flat_rows - average
    inverse_deviation = lax.rsqrt(
        jnp.mean(centered_input * centered_input, axis=-1, keepdims=True) + norm_epsilon
    )
    standardized_rows = centered_input * inverse_deviation
    normalized_rows = (standardized_rows * layer_norm_gain).astype(jnp.bfloat16)
    projected = jnp.dot(normalized_rows, qkv_full, preferred_element_type=jnp.float32).astype(
        jnp.bfloat16
    )
    head_shape = (window_count, cell_count, head_count, head_size)
    query_rows = projected[:, :inner_width].reshape(head_shape)
    key_vectors = projected[:, inner_width : 2 * inner_width].reshape(head_shape)
    value_rows = projected[:, 2 * inner_width :].reshape(head_shape)
    scores = (
        jnp.einsum("wmhd,wnhd->whmn", query_rows, key_vectors, preferred_element_type=jnp.float32)
        * score_scale
        + bias_full[None]
    )
    same_region = labels[:, None, :, None] == labels[:, None, None, :]
    scores = jnp.where(same_region, scores, -1e30)
    row_peak = jnp.max(scores, axis=-1, keepdims=True)
    exp_scores = jnp.exp(scores - row_peak)
    attention_weights = exp_scores / jnp.sum(exp_scores, axis=-1, keepdims=True)
    reduced_probability = attention_weights.astype(jnp.bfloat16)
    attended = jnp.einsum(
        "whmn,wnhd->wmhd", reduced_probability, value_rows, preferred_element_type=jnp.float32
    ).astype(jnp.bfloat16)
    stored_residuals = (
        standardized_rows,
        inverse_deviation,
        query_rows,
        key_vectors,
        value_rows,
        attention_weights,
        reduced_probability,
    )
    return (stored_residuals, attended.reshape(-1, inner_width))


def attend_backward(stored_residuals, d_attended, layer_norm_gain, qkv_full):
    (
        standardized_rows,
        inverse_deviation,
        query_rows,
        key_vectors,
        value_rows,
        attention_weights,
        reduced_probability,
    ) = stored_residuals
    head_shape = query_rows.shape
    score_scale = head_shape[3] ** (-0.5)
    total_row_count = standardized_rows.shape[0]
    inner_width = head_shape[2] * head_shape[3]
    d_heads = d_attended.reshape(head_shape)
    d_prob = jnp.einsum("wmhd,wnhd->whmn", d_heads, value_rows, preferred_element_type=jnp.float32)
    d_values = jnp.einsum(
        "whmn,wmhd->wnhd", reduced_probability, d_heads, preferred_element_type=jnp.float32
    ).astype(jnp.bfloat16)
    d_scores = attention_weights * (
        d_prob - jnp.sum(attention_weights * d_prob, axis=-1, keepdims=True)
    )
    table_part = jnp.sum(d_scores, axis=0)
    d_low = d_scores.astype(jnp.bfloat16)
    d_queries = (
        jnp.einsum("whmn,wnhd->wmhd", d_low, key_vectors, preferred_element_type=jnp.float32)
        * score_scale
    ).astype(jnp.bfloat16)
    d_keys = (
        jnp.einsum("whmn,wmhd->wnhd", d_low, query_rows, preferred_element_type=jnp.float32)
        * score_scale
    ).astype(jnp.bfloat16)
    d_projected = jnp.concatenate(
        [
            d_queries.reshape(total_row_count, inner_width),
            d_keys.reshape(total_row_count, inner_width),
            d_values.reshape(total_row_count, inner_width),
        ],
        axis=1,
    )
    normalized_gradient = lax.dot_general(
        d_projected, qkv_full, (((1,), (1,)), ((), ())), preferred_element_type=jnp.float32
    )
    gain_contribution = jnp.sum(normalized_gradient * standardized_rows, axis=0)
    scaled_rows = normalized_gradient * layer_norm_gain
    branch_gradient = inverse_deviation * (
        scaled_rows
        - jnp.mean(scaled_rows, axis=-1, keepdims=True)
        - standardized_rows * jnp.mean(scaled_rows * standardized_rows, axis=-1, keepdims=True)
    )
    return (branch_gradient.astype(jnp.bfloat16), gain_contribution, table_part)


def on_device(
    pixels,
    cotangent,
    embed_weight,
    embed_bias,
    layer_norm_gain,
    qkv_weight,
    out_weight,
    bias_table,
    rel_index,
    shifts,
):
    images, rows_dev, cols_dev, features = cotangent.shape
    head_count = bias_table.shape[0]
    grid_rows = rows_dev * lax.axis_size("row")
    grid_cols = cols_dev * lax.axis_size("col")
    row_shift = shifts[:, 0]
    col_shift = shifts[:, 1]
    qkv_rowwise = lax.all_gather(qkv_weight, "row", axis=0, tiled=True)
    qkv_full, out_columns = (
        lax.all_gather(qkv_rowwise, ("col", "dp"), axis=1, tiled=True),
        lax.all_gather(out_weight, ("col", "dp"), axis=1, tiled=True),
    )
    patches = make_patches(pixels)
    tokens = embed_cells(patches, embed_weight, embed_bias)
    below = from_behind((tokens, cotangent), "row", -1)
    shifted = splice_after(tokens, below[0], row_shift, 1)
    shifted_cot = splice_after(cotangent, below[1], row_shift, 1)
    beside = from_behind((shifted[:, :, :WIN], shifted_cot[:, :, :WIN]), "col", -1)
    shifted = splice_after(shifted, beside[0], col_shift, 2)
    shifted_cot = splice_after(shifted_cot, beside[1], col_shift, 2)
    row_ids = lax.axis_index("row") * rows_dev + jnp.arange(rows_dev, dtype=jnp.int32)
    col_ids = lax.axis_index("col") * cols_dev + jnp.arange(cols_dev, dtype=jnp.int32)
    row_part = (row_ids[None, :] >= grid_rows - row_shift[:, None]).astype(jnp.int32)
    col_part = (col_ids[None, :] >= grid_cols - col_shift[:, None]).astype(jnp.int32)
    region = 2 * row_part[:, :, None] + col_part[:, None, :]
    labels = window_split(region.reshape(images * rows_dev, cols_dev, 1))[:, :, 0]
    cell_windows = window_split(shifted.reshape(images * rows_dev, cols_dev, features))
    cot_flat = window_split(shifted_cot.reshape(images * rows_dev, cols_dev, features)).reshape(
        -1, features
    )
    selector = (
        rel_index.reshape(-1)[:, None] == jnp.arange(bias_table.shape[1], dtype=jnp.int32)[None, :]
    ).astype(jnp.float32)
    bias_full = jnp.dot(selector, bias_table.T, precision=lax.Precision.HIGHEST).T.reshape(
        head_count, WIN * WIN, WIN * WIN
    )
    stored_residuals, attended = attend_forward(
        cell_windows, labels, layer_norm_gain, qkv_full, bias_full
    )
    d_attended = lax.dot_general(
        cot_flat,
        lax.all_gather(out_columns, "row", axis=0, tiled=True),
        (((1,), (1,)), ((), ())),
        preferred_element_type=jnp.float32,
    ).astype(jnp.bfloat16)
    partial_rows = lax.psum_scatter(
        lax.dot_general(
            attended, cot_flat, (((0,), (0,)), ((), ())), preferred_element_type=jnp.float32
        ),
        "row",
        scatter_dimension=0,
        tiled=True,
    )
    out_weight_grad = lax.psum_scatter(partial_rows, ("col", "dp"), scatter_dimension=1, tiled=True)
    d_rows, gain_contribution, table_part = attend_backward(
        stored_residuals, d_attended, layer_norm_gain, qkv_full
    )
    branch_gradient = window_join(
        d_rows.reshape(-1, WIN * WIN, features), images * rows_dev, cols_dev
    ).reshape(images, rows_dev, cols_dev, features)
    patch_rows = patches.reshape(-1, patches.shape[-1])
    cot_rows = cotangent.reshape(-1, features)
    contract = (((0,), (0,)), ((), ()))
    behind = from_behind(branch_gradient[:, :, cols_dev - WIN :], "col", 1)
    d_back = splice_before(branch_gradient, behind, col_shift, 2)
    above = from_behind(d_back, "row", 1)
    d_back = splice_before(d_back, above, row_shift, 1)
    back_rows = d_back.reshape(-1, features)
    embed_grad = lax.dot_general(
        patch_rows, cot_rows, contract, preferred_element_type=jnp.float32
    ) + lax.dot_general(patch_rows, back_rows, contract, preferred_element_type=jnp.float32)
    bias_grad = jnp.sum(cot_rows, axis=0, dtype=jnp.float32) + jnp.sum(
        back_rows, axis=0, dtype=jnp.float32
    )
    table_grad = jnp.dot(
        table_part.reshape(head_count, -1), selector, precision=lax.Precision.HIGHEST
    )
    totals = lax.psum((embed_grad, bias_grad, gain_contribution, table_grad), ("row", "col", "dp"))
    return (out_weight_grad, totals[0], totals[1], totals[2], totals[3])


def solution(mesh):
    return jax.shard_map(
        on_device,
        mesh=mesh,
        in_specs=(
            P("dp", None, "row", "col"),
            P("dp", "row", "col", None),
            P(),
            P(),
            P(),
            P("row", ("col", "dp")),
            P("row", ("col", "dp")),
            P(),
            P(),
            P("dp", None),
        ),
        out_specs=(P("row", ("col", "dp")), P(), P(), P(), P()),
        check_vma=False,
    )
```

profile of v0, /device:TPU:0, one launch (start us, length us, event | category | flops | bytes accessed | tf_op | source)
XLA Modules:
  0.0 390.5 jit_solution(13253919688802146951)
XLA Ops:
  8.0 45.2 %all-gather.4.cloned.1.call-done = bf16[1024,576]{0,1:T(8,128)(2,1)} async-done(((bf16[128,576]{0,1:T(8,128)(2,1)}), bf16[1024,576]{0,1:T(8,128)(2,1)}) %all-gather.4.cloned.1.call-update) | async-done | bytes 1179664 | tf_op jit(solution)/shard_map/all_gather | solution.py:184
  55.4 2.4 reshape.177
  60.0 12.5 %all_gather.14 = bf16[96,1024]{1,0:T(8,128)(2,1)} all-gather(bf16[96,256]{1,0:T(8,128)(2,1)S(1)} %copy-done.13), channel_id=1, replica_groups=mesh['row'=8,'col'=2,'dp'=2] {'col','dp'}, dimensions={1}, use_global_device_ids=true | all-gather | bytes 245760 | tf_op jit(solution)/shard_map/all_gather | solution.py:187
  76.8 2.6 convolution_bitcast_fusion
  86.7 7.0 %all-gather.6.cloned.1.call-done = bf16[1024,2304]{0,1:T(8,128)(2,1)} async-done(((bf16[1024,576]{0,1:T(8,128)(2,1)}), bf16[1024,2304]{0,1:T(8,128)(2,1)}) %all-gather.6.cloned.1.call-update) | async-done | bytes 4718608 | tf_op jit(solution)/shard_map/all_gather | solution.py:186
  93.7 3.8 convolution_convert_fusion
  99.9 2.5 reshape.366
  109.0 3.8 fusion.7
  112.7 2.7 copy.168
  115.4 2.5 reshape.182
  117.9 3.4 fusion.46
  121.5 17.9 %all-gather.8.cloned.1.call-done = bf16[768,1024]{1,0:T(8,128)(2,1)} async-done(((bf16[96,1024]{1,0:T(8,128)(2,1)}), bf16[768,1024]{1,0:T(8,128)(2,1)}) %all-gather.8.cloned.1.call-update) | async-done | bytes 1572880 | tf_op jit(solution)/shard_map/all_gather | solution.py:218
  139.4 3.0 convolution_convert_fusion.3
  142.4 2.4 reshape.369
  144.8 2.5 copy.182
  147.3 2.8 multiply_reduce_fusion
  156.0 2.5 reshape.185
  162.8 3.5 fusion.8
  169.3 4.2 %multiply_reduce_fusion.1 = (f32[1024]{0:T(1024)S(1)}, f32[256]{0:T(256)S(1)}, f32[256]{0:T(256)S(1)}, f32[256,1024]{1,0:T(8,128)S(1)}) fusion(f32[1,4,8,8,1024]{4,3,2,1,0:T(8,128)S(1)} %copy.156, f32[256]{0:T(256)S(1)} %rsqrt.12, f32[256]{0:T(256)S(1)} %div.23, f32[1024]{0:T(1024)S(1)} %copy-done.15, bf16[1024,2304]{0,1:T(8,128)(2,1)} %all-gather.6.cloned.1.call-done, ...), kind=kOutput, calls=%fused_computation.41 | convolution fusion | flops 1213594112 | bytes 8007680 | tf_op jit(solution)/shard_map/dot_general | solution.py:153
  177.6 15.2 %collective-permute-done.5 = bf16[1,8,32,1024]{3,2,1,0:T(8,128)(2,1)S(1)} collective-permute-done((bf16[1,8,32,1024]{3,2,1,0:T(8,128)(2,1)S(1)}, bf16[1,8,32,1024]{3,2,1,0:T(8,128)(2,1)S(1)}, u32[]{:S(2)}, u32[]{:S(2)}) %collective-permute-start.5) | collective-permute-done | bytes 524320 | tf_op jit(solution)/shard_map/ppermute | solution.py:14
  194.0 33.6 %reduce-scatter.3.cloned.1.call-done = f32[96,1024]{1,0:T(8,128)} async-done(((f32[768,1024]{1,0:T(8,128)}), f32[96,1024]{1,0:T(8,128)}) %reduce-scatter.3.cloned.1.call-update) | async-done | bytes 393232 | tf_op jit(solution)/shard_map/reduce_scatter | solution.py:222
  229.5 40.2 %all-reduce.2 = (f32[1024]{0:T(1024)}, f32[1024]{0:T(1024)}, f32[12,225]{1,0:T(8,128)}) all-reduce(f32[1024]{0:T(1024)S(1)} %add.134, f32[1024]{0:T(1024)S(1)} %get-tuple-element.71, f32[12,225]{1,0:T(8,128)S(1)} %fusion.1), channel_id=1, replica_groups=mesh['row'=8,'col'=2,'dp'=2] {'row','col','dp'}, use_global_device_ids=true, to_apply=%region_12.13 | all-reduce | flops 4748 | bytes 37984 | tf_op jit(solution)/shard_map/psum | solution.py:254
  269.7 87.6 %all-reduce.5.cloned.1.call-done = f32[48,1024]{1,0:T(8,128)} async-done(((f32[48,1024]{1,0:T(8,128)}), f32[48,1024]{1,0:T(8,128)}) %all-reduce.5.cloned.1.call-update) | async-done | bytes 196624 | tf_op jit(solution)/shard_map/psum | solution.py:254
  357.4 24.7 %reduce-scatter.5.cloned.1.call-done = f32[96,256]{1,0:T(8,128)} async-done(((f32[96,1024]{1,0:T(8,128)}), f32[96,256]{1,0:T(8,128)}) %reduce-scatter.5.cloned.1.call-update) | async-done | bytes 98320 | tf_op jit(solution)/shard_map/reduce_scatter | solution.py:230
  (121 shorter events, 39.7 us)
Async XLA Ops:
  7.2 51.3 %copy-start = (bf16[48,1024]{1,0:T(8,128)(2,1)S(1)}, bf16[48,1024]{1,0:T(8,128)(2,1)}, u32[]{:S(2)}) copy-start(bf16[48,1024]{1,0:T(8,128)(2,1)} %param.12) | copy-start | bytes 294916
  7.2 51.3 %copy-start.18 = (f32[1024]{0:T(1024)S(1)}, f32[1024]{0:T(1024)}, u32[]{:S(2)}) copy-start(f32[1024]{0:T(1024)} %param.13) | copy-start | bytes 12292
  7.2 45.9 %all-gather.4.cloned.1.call-start = ((), (), s32[]{:S(2)}) async-start(), calls=%async_computation.2 | async-start | bytes 1327104 | tf_op jit(solution)/shard_map/all_gather | solution.py:184
  7.9 85.8 %all-gather.6.cloned.1.call-start = ((), (), s32[]{:S(2)}) async-start(), calls=%async_computation.3 | async-start | bytes 5898240 | tf_op jit(solution)/shard_map/all_gather | solution.py:186
  53.1 6.9 %copy-start.13 = (bf16[96,256]{1,0:T(8,128)(2,1)S(1)}, bf16[96,256]{1,0:T(8,128)(2,1)}, u32[]{:S(2)}) copy-start(bf16[96,256]{1,0:T(8,128)(2,1)} %param.16) | copy-start | bytes 147460
  53.2 19.5 %copy-start.19 = (s32[1,2]{1,0:T(1,128)S(1)}, s32[1,2]{1,0:T(1,128)}, u32[]{:S(2)}) copy-start(s32[1,2]{1,0:T(1,128)} %param.19) | copy-start | bytes 28
  53.2 22.8 %copy-start.14 = (s32[64,64]{1,0:T(8,128)S(1)}, s32[64,64]{1,0:T(8,128)}, u32[]{:S(2)}) copy-start(s32[64,64]{1,0:T(8,128)} %param.18) | copy-start | bytes 49156
  53.2 23.6 %copy-start.20 = (f32[12,225]{1,0:T(8,128)S(1)}, f32[12,225]{1,0:T(8,128)}, u32[]{:S(2)}) copy-start(f32[12,225]{1,0:T(8,128)} %param.17) | copy-start | bytes 32404
  53.2 86.2 %all-gather.8.cloned.1.call-start = ((), (), s32[]{:S(2)}) async-start(), calls=%async_computation.6 | async-start | bytes 1769472 | tf_op jit(solution)/shard_map/all_gather | solution.py:218
  53.2 29.6 %collective-permute-start.2 = (bf16[1,8,32,1024]{3,2,1,0:T(8,128)(2,1)}, bf16[1,8,32,1024]{3,2,1,0:T(8,128)(2,1)S(1)}, u32[]{:S(2)}, u32[]{:S(2)}) collective-permute-start(bf16[1,8,32,1024]{3,2,1,0:T(8,128)(2,1)} %param.11), channel_id=1, source_target_pairs={{0,28},{4,0},{8,4},{12,8},{16,12},{20,16},{24,20},{28,24},{1,29},{... | collective-permute-start | bytes 1572872 | tf_op jit(solution)/shard_map/ppermute | solution.py:14
  58.5 20.9 %copy-start.8 = (bf16[1,8,32,3,4,4]{2,1,5,4,3,0:T(8,128)(2,1)}, bf16[1,8,32,3,4,4]{2,1,5,4,3,0:T(8,128)(2,1)S(1)}, u32[]{:S(2)}) copy-start(bf16[1,8,32,3,4,4]{2,1,5,4,3,0:T(8,128)(2,1)S(1)} %copy.154) | copy-start | bytes 73732
  58.8 20.5 %collective-permute-start = (bf16[1,8,32,1024]{3,2,1,0:T(8,128)(2,1)S(1)}, bf16[1,8,32,1024]{3,2,1,0:T(8,128)(2,1)S(1)}, u32[]{:S(2)}, u32[]{:S(2)}) collective-permute-start(bf16[1,8,32,1024]{3,2,1,0:T(8,128)(2,1)S(1)} %fusion.11), channel_id=1, source_target_pairs={{0,28},{4,0},{8,4},{12,8},{16,12},{20,16},{24,20},{28,24},{1,29},{... | collective-permute-start | bytes 1572872 | tf_op jit(solution)/shard_map/ppermute | solution.py:14
  72.6 155.0 %reduce-scatter.3.cloned.1.call-start = ((), (), s32[]{:S(2)}) async-start(), calls=%async_computation.4 | async-start | bytes 3538944 | tf_op jit(solution)/shard_map/reduce_scatter | solution.py:222
  76.1 3.3 copy-start.16
  79.4 3.5 copy-start.5
  79.6 4.0 %collective-permute-start.1 = (bf16[1,8,8,1024]{3,2,1,0:T(8,128)(2,1)S(1)}, bf16[1,8,8,1024]{3,2,1,0:T(8,128)(2,1)S(1)}, u32[]{:S(2)}, u32[]{:S(2)}) collective-permute-start(bf16[1,8,8,1024]{3,2,1,0:T(8,128)(2,1)S(1)} %slice.150), channel_id=1, source_target_pairs={{0,2},{2,0},{1,3},{3,1},{4,6},{6,4},{5,7},{7,5},{8,10},{10,8},{9,1... | collective-permute-start | bytes 393224 | tf_op jit(solution)/shard_map/ppermute | solution.py:14
  83.1 1.5 collective-permute-start.3
  121.3 236.1 %all-reduce.5.cloned.1.call-start = ((), (), s32[]{:S(2)}) async-start(), calls=%async_computation.7 | async-start | bytes 393216 | tf_op jit(solution)/shard_map/psum | solution.py:254
  153.8 4.8 %copy-start.2 = (bf16[4,12,64,64]{2,3,1,0:T(8,128)(2,1)S(1)}, bf16[4,12,64,64]{2,3,1,0:T(8,128)(2,1)}, u32[]{:S(2)}) copy-start(bf16[4,12,64,64]{2,3,1,0:T(8,128)(2,1)} %copy-done.1) | copy-start | bytes 1179652
  174.0 1.4 collective-permute-start.4
  175.6 17.2 %collective-permute-start.5 = (bf16[1,8,32,1024]{3,2,1,0:T(8,128)(2,1)S(1)}, bf16[1,8,32,1024]{3,2,1,0:T(8,128)(2,1)S(1)}, u32[]{:S(2)}, u32[]{:S(2)}) collective-permute-start(bf16[1,8,32,1024]{3,2,1,0:T(8,128)(2,1)S(1)} %fusion.25), channel_id=1, source_target_pairs={{0,4},{4,8},{8,12},{12,16},{16,20},{20,24},{24,28},{28,0},{1,5},{5... | collective-permute-start | bytes 1572872 | tf_op jit(solution)/shard_map/ppermute | solution.py:14
  192.7 35.0 %copy-start.6 = (f32[12,64,64]{1,2,0:T(8,128)S(1)}, f32[12,64,64]{1,2,0:T(8,128)}, u32[]{:S(2)}) copy-start(f32[12,64,64]{1,2,0:T(8,128)} %get-tuple-element.81) | copy-start | bytes 589828
  193.0 35.0 %copy-start.17 = (s32[4096]{0:T(1024)S(1)}, s32[4096]{0:T(1024)}, u32[]{:S(2)}) copy-start(s32[4096]{0:T(1024)} %copy-done.16) | copy-start | bytes 49156
  193.9 188.1 %reduce-scatter.5.cloned.1.call-start = ((), (), s32[]{:S(2)}) async-start(), calls=%async_computation.5 | async-start | bytes 491520 | tf_op jit(solution)/shard_map/reduce_scatter | solution.py:230
  (9 other events, 20.3 us)
Sparse Core Ops, SparseCore 0:
  10.0 43.0 all-gather.3
  54.7 38.9 all-gather.5
  95.9 43.4 all-gather.7
  142.9 84.6 reduce-scatter.2
  233.6 123.7 all-reduce.4
  360.3 21.7 reduce-scatter.4
where the time goes:
time: 391 us
  waiting for transfers between devices  233 us (60%)
  blocking collectives  52.7 us (13%)
  local copies, waits for them, and re-layouts  38.4 us (10%)
  matrix products  34.1 us (9%)
  between operations  22.4 us (6%)
  other arithmetic  5.59 us (1%)
  starting transfers between devices  4.81 us (1%)
    psum x1, waiting for transfers between devices, on_device(): lax.psum((embed_grad, bias_grad, gain_contribution, table_grad), ('row',...  87.6 us
    all_gather x1, waiting for transfers between devices, on_device(): qkv_rowwise = lax.all_gather(qkv_weight, 'row', axis=0, tiled=True)  45.2 us
    psum x1, blocking collectives, on_device(): lax.psum((embed_grad, bias_grad, gain_contribution, table_grad), ('row',...  40.2 us
    reduce_scatter x1, waiting for transfers between devices, on_device(): lax.psum_scatter(lax.dot_general(attended, cot_flat, (((0,), (0,)), ((),...  33.6 us
    reduce_scatter x1, waiting for transfers between devices, on_device(): lax.psum_scatter(partial_rows, ('col', 'dp'), scatter_dimension=1, tiled=...  24.7 us
    all_gather x1, waiting for transfers between devices, on_device(): lax.all_gather(out_columns, 'row', axis=0, tiled=True)  17.9 us
    ppermute x6, waiting for transfers between devices, from_behind(): return lax.ppermute(value, axis, pairs)  15.7 us
    all_gather x1, blocking collectives, on_device(): lax.all_gather(out_weight, ('col', 'dp'), axis=1, tiled=True)  12.5 us
  transfers between devices with their start and end apart: 12, of which 8 were waited for; matrix products, arithmetic and copies ran while one was open for 19% of the time, Pallas kernels for 0%

commit v1 on v0

--- a/solution.py
+++ b/solution.py
@@ -6,6 +6,11 @@
 WIN = 8
 PATCH = 4
 norm_epsilon = 1e-05
+
+
+def by_each_axis(value_2, one, other):
+    half = lax.psum(value_2, one)
+    return lax.psum(half, other)
 
 
 def from_behind(value, axis, steps):
@@ -251,7 +256,9 @@
     table_grad = jnp.dot(
         table_part.reshape(head_count, -1), selector, precision=lax.Precision.HIGHEST
     )
-    totals = lax.psum((embed_grad, bias_grad, gain_contribution, table_grad), ("row", "col", "dp"))
+    totals = by_each_axis(
+        (embed_grad, bias_grad, gain_contribution, table_grad), "row", ("col", "dp")
+    )
     return (out_weight_grad, totals[0], totals[1], totals[2], totals[3])
 
 

time: 391 us -> 414 us (1.059)
  waiting for transfers between devices: 233 us -> 256 us
  local copies, waits for them, and re-layouts: 38.4 us -> 26.7 us
  blocking collectives: 52.7 us -> 62.1 us
    reduce_scatter x1, waiting for transfers between devices: 33.6 us -> 76.8 us  [on_device(): lax.psum_scatter(lax.dot_general(attended, cot_flat, (((0,), (0,)), ((),...]
    all_gather x1, waiting for transfers between devices: 7.04 us -> 31.3 us  [on_device(): lax.all_gather(qkv_rowwise, ('col', 'dp'), axis=1, tiled=True)]
    psum x1 -> x2, waiting for transfers between devices: 87.6 us -> 65.8 us  [the longest x1 65.8 us: by_each_axis(): half = lax.psum(value_2, one)]
    reduce_scatter x1, waiting for transfers between devices: 24.7 us -> 6.67 us  [on_device(): lax.psum_scatter(partial_rows, ('col', 'dp'), scatter_dimension=1, tiled=...]
    all_gather x1, waiting for transfers between devices: 45.2 us -> 31.7 us  [on_device(): qkv_rowwise = lax.all_gather(qkv_weight, 'row', axis=0, tiled=True)]
    ppermute x6, waiting for transfers between devices: 15.7 us -> 25.1 us  [from_behind(): return lax.ppermute(value, axis, pairs)]
    psum x1 -> x2, blocking collectives: 40.2 us -> 48.7 us  [the longest x1 35.3 us: by_each_axis(): half = lax.psum(value_2, one)]
  transfers between devices with their start and end apart: 12 -> 13, of which waited for: 8 -> 9; matrix products, arithmetic and copies ran while one was open for 19% -> 6% of each run, Pallas kernels for 0% -> 0%
where the time goes in v1:
time: 414 us; the launch traced here: 413 us
  waiting for transfers between devices  256 us (62%)
  blocking collectives  62.1 us (15%)
  matrix products  32.4 us (8%)
  local copies, waits for them, and re-layouts  26.7 us (6%)
  between operations  22.4 us (5%)
  other arithmetic  7.36 us (2%)
  starting transfers between devices  6.07 us (1%)
    reduce_scatter x1, waiting for transfers between devices, on_device(): lax.psum_scatter(lax.dot_general(attended, cot_flat, (((0,), (0,)), ((),...  76.8 us
    psum x1, waiting for transfers between devices, by_each_axis(): half = lax.psum(value_2, one)  65.8 us
    psum x1, blocking collectives, by_each_axis(): half = lax.psum(value_2, one)  35.3 us
    all_gather x1, waiting for transfers between devices, on_device(): qkv_rowwise = lax.all_gather(qkv_weight, 'row', axis=0, tiled=True)  31.7 us
    all_gather x1, waiting for transfers between devices, on_device(): lax.all_gather(qkv_rowwise, ('col', 'dp'), axis=1, tiled=True)  31.3 us
    ppermute x6, waiting for transfers between devices, from_behind(): return lax.ppermute(value, axis, pairs)  25.1 us
    all_gather x1, waiting for transfers between devices, on_device(): lax.all_gather(out_columns, 'row', axis=0, tiled=True)  17.7 us
    all_gather x1, blocking collectives, on_device(): lax.all_gather(out_weight, ('col', 'dp'), axis=1, tiled=True)  13.4 us
  transfers between devices with their start and end apart: 13, of which 9 were waited for; matrix products, arithmetic and copies ran while one was open for 6% of the time, Pallas kernels for 0%

profile of v1, /device:TPU:0, one launch (start us, length us, event | category | flops | bytes accessed | tf_op | source)
XLA Modules:
  0.0 412.8 jit_solution(13182960756329515878)
XLA Ops:
  8.0 13.4 %all_gather.14 = bf16[96,1024]{1,0:T(8,128)(2,1)} all-gather(bf16[96,256]{1,0:T(8,128)(2,1)} %param.16), channel_id=1, replica_groups=mesh['row'=8,'col'=2,'dp'=2] {'col','dp'}, dimensions={1}, use_global_device_ids=true | all-gather | bytes 245760 | tf_op jit(solution)/shard_map/all_gather | solution.py:192
  21.5 31.7 %all-gather.4.cloned.1.call-done = bf16[1024,576]{0,1:T(8,128)(2,1)} async-done(((bf16[128,576]{0,1:T(8,128)(2,1)}), bf16[1024,576]{0,1:T(8,128)(2,1)}) %all-gather.4.cloned.1.call-update) | async-done | bytes 1179664 | tf_op jit(solution)/shard_map/all_gather | solution.py:189
  53.2 2.1 collective-permute-start.2
  63.4 2.6 convolution_bitcast_fusion
  66.0 16.5 %collective-permute-done = bf16[1,8,32,1024]{3,2,1,0:T(8,128)(2,1)S(1)} collective-permute-done((bf16[1,8,32,1024]{3,2,1,0:T(8,128)(2,1)S(1)}, bf16[1,8,32,1024]{3,2,1,0:T(8,128)(2,1)S(1)}, u32[]{:S(2)}, u32[]{:S(2)}) %collective-permute-start) | collective-permute-done | bytes 524320 | tf_op jit(solution)/shard_map/ppermute | solution.py:19
  89.8 17.7 %all-gather.8.cloned.1.call-done = bf16[768,1024]{1,0:T(8,128)(2,1)} async-done(((bf16[96,1024]{1,0:T(8,128)(2,1)}), bf16[768,1024]{1,0:T(8,128)(2,1)}) %all-gather.8.cloned.1.call-update) | async-done | bytes 1572880 | tf_op jit(solution)/shard_map/all_gather | solution.py:223
  107.5 2.8 convolution_convert_fusion.3
  113.5 31.3 %all-gather.6.cloned.1.call-done = bf16[1024,2304]{0,1:T(8,128)(2,1)} async-done(((bf16[1024,576]{0,1:T(8,128)(2,1)}), bf16[1024,2304]{0,1:T(8,128)(2,1)}) %all-gather.6.cloned.1.call-update) | async-done | bytes 4718608 | tf_op jit(solution)/shard_map/all_gather | solution.py:191
  144.9 3.8 convolution_convert_fusion
  151.1 2.6 reshape.366
  155.3 1.8 copy.178
  160.2 3.6 fusion.8
  163.8 2.6 multiply_reduce_fusion
  170.6 1.8 copy.177
  176.5 4.2 %multiply_reduce_fusion.1 = (f32[1024]{0:T(1024)S(1)}, f32[256]{0:T(256)S(1)}, f32[256]{0:T(256)S(1)}, f32[256,1024]{1,0:T(8,128)S(1)}) fusion(f32[1,4,8,8,1024]{4,3,2,1,0:T(8,128)S(1)} %copy.156, f32[256]{0:T(256)S(1)} %rsqrt.12, f32[256]{0:T(256)S(1)} %div.23, f32[1024]{0:T(1024)S(1)} %copy-done.16, bf16[1024,2304]{0,1:T(8,128)(2,1)} %all-gather.6.cloned.1.call-done, ...), kind=kOutput, calls=%fused_computation.41 | convolution fusion | flops 1213594112 | bytes 8007680 | tf_op jit(solution)/shard_map/dot_general | solution.py:158
  186.2 3.5 fusion.7
  189.7 1.8 copy.168
  191.9 8.1 %collective-permute-done.5 = bf16[1,8,32,1024]{3,2,1,0:T(8,128)(2,1)} collective-permute-done((bf16[1,8,32,1024]{3,2,1,0:T(8,128)(2,1)S(1)}, bf16[1,8,32,1024]{3,2,1,0:T(8,128)(2,1)}, u32[]{:S(2)}, u32[]{:S(2)}) %collective-permute-start.5) | collective-permute-done | bytes 524320 | tf_op jit(solution)/shard_map/ppermute | solution.py:19
  202.2 2.2 fusion.46
  204.5 65.8 %all-reduce.7.cloned.1.call-done = f32[48,1024]{1,0:T(8,128)} async-done(((f32[48,1024]{1,0:T(8,128)}), f32[48,1024]{1,0:T(8,128)}) %all-reduce.7.cloned.1.call-update) | async-done | bytes 196624 | tf_op jit(solution)/shard_map/psum | solution.py:12
  270.3 76.8 %reduce-scatter.3.cloned.1.call-done = f32[96,1024]{1,0:T(8,128)} async-done(((f32[768,1024]{1,0:T(8,128)}), f32[96,1024]{1,0:T(8,128)}) %reduce-scatter.3.cloned.1.call-update) | async-done | bytes 393232 | tf_op jit(solution)/shard_map/reduce_scatter | solution.py:227
  349.0 35.3 %all-reduce.2 = (f32[1024]{0:T(1024)S(1)}, f32[1024]{0:T(1024)S(1)}, f32[12,225]{1,0:T(8,128)S(1)}) all-reduce(f32[1024]{0:T(1024)S(1)} %add.142, f32[1024]{0:T(1024)S(1)} %get-tuple-element.71, f32[12,225]{1,0:T(8,128)S(1)} %fusion.1), channel_id=1, replica_groups=mesh['row'=8,'col'=2,'dp'=2] {'row'}, use_global_device_ids=true, to_apply=%region_13.14 | all-reduce | flops 4748 | bytes 37984 | tf_op jit(solution)/shard_map/psum | solution.py:12
  384.3 13.4 %all-reduce.3 = (f32[1024]{0:T(1024)}, f32[1024]{0:T(1024)}, f32[12,225]{1,0:T(8,128)}) all-reduce(f32[1024]{0:T(1024)S(1)} %get-tuple-element.74, f32[1024]{0:T(1024)S(1)} %get-tuple-element.75, f32[12,225]{1,0:T(8,128)S(1)} %get-tuple-element.76), channel_id=1, replica_groups=mesh['row'=8,'col'=2,'dp'=2] {'col','dp'}, use_global_device_ids=true, to_apply=%region_14.15 | all-reduce | flops 4748 | bytes 37984 | tf_op jit(solution)/shard_map/psum | solution.py:13
  397.7 6.7 %reduce-scatter.5.cloned.1.call-done = f32[96,256]{1,0:T(8,128)} async-done(((f32[96,1024]{1,0:T(8,128)}), f32[96,256]{1,0:T(8,128)}) %reduce-scatter.5.cloned.1.call-update) | async-done | bytes 98320 | tf_op jit(solution)/shard_map/reduce_scatter | solution.py:235
  (127 shorter events, 38.6 us)
Async XLA Ops:
  7.2 50.6 %copy-start = (bf16[48,1024]{1,0:T(8,128)(2,1)S(1)}, bf16[48,1024]{1,0:T(8,128)(2,1)}, u32[]{:S(2)}) copy-start(bf16[48,1024]{1,0:T(8,128)(2,1)} %param.12) | copy-start | bytes 294916
  7.2 46.0 %copy-start.3 = (bf16[1,8,32,1024]{3,2,1,0:T(8,128)(2,1)S(1)}, bf16[1,8,32,1024]{3,2,1,0:T(8,128)(2,1)}, u32[]{:S(2)}) copy-start(bf16[1,8,32,1024]{3,2,1,0:T(8,128)(2,1)} %param.11) | copy-start | bytes 1572868
  7.2 48.2 %copy-start.15 = (bf16[1,3,32,128]{3,2,1,0:T(8,128)(2,1)S(1)}, bf16[1,3,32,128]{3,2,1,0:T(8,128)(2,1)}, u32[]{:S(2)}) copy-start(bf16[1,3,32,128]{3,2,1,0:T(8,128)(2,1)} %param.10) | copy-start | bytes 73732
  7.2 45.9 %all-gather.4.cloned.1.call-start = ((), (), s32[]{:S(2)}) async-start(), calls=%async_computation.2 | async-start | bytes 1327104 | tf_op jit(solution)/shard_map/all_gather | solution.py:189
  7.9 99.5 %all-gather.8.cloned.1.call-start = ((), (), s32[]{:S(2)}) async-start(), calls=%async_computation.6 | async-start | bytes 1769472 | tf_op jit(solution)/shard_map/all_gather | solution.py:223
  21.4 36.4 %copy-start.19 = (f32[1024]{0:T(1024)S(1)}, f32[1024]{0:T(1024)}, u32[]{:S(2)}) copy-start(f32[1024]{0:T(1024)} %param.13) | copy-start | bytes 12292
  21.4 123.4 %all-gather.6.cloned.1.call-start = ((), (), s32[]{:S(2)}) async-start(), calls=%async_computation.3 | async-start | bytes 5898240 | tf_op jit(solution)/shard_map/all_gather | solution.py:191
  53.2 217.1 %all-reduce.7.cloned.1.call-start = ((), (), s32[]{:S(2)}) async-start(), calls=%async_computation.7 | async-start | bytes 393216 | tf_op jit(solution)/shard_map/psum | solution.py:12
  53.2 32.7 %collective-permute-start.2 = (bf16[1,8,32,1024]{3,2,1,0:T(8,128)(2,1)S(1)}, bf16[1,8,32,1024]{3,2,1,0:T(8,128)(2,1)S(1)}, u32[]{:S(2)}, u32[]{:S(2)}) collective-permute-start(bf16[1,8,32,1024]{3,2,1,0:T(8,128)(2,1)S(1)} %copy-done.3), channel_id=1, source_target_pairs={{0,28},{4,0},{8,4},{12,8},{16,12},{20,16},{24,20},{28,24},{1,29},{... | collective-permute-start | bytes 1572872 | tf_op jit(solution)/shard_map/ppermute | solution.py:19
  57.8 24.9 %copy-start.10 = (bf16[1,8,32,3,4,4]{2,1,5,4,3,0:T(8,128)(2,1)}, bf16[1,8,32,3,4,4]{2,1,5,4,3,0:T(8,128)(2,1)S(1)}, u32[]{:S(2)}) copy-start(bf16[1,8,32,3,4,4]{2,1,5,4,3,0:T(8,128)(2,1)S(1)} %copy.154) | copy-start | bytes 73732
  58.1 24.4 %collective-permute-start = (bf16[1,8,32,1024]{3,2,1,0:T(8,128)(2,1)S(1)}, bf16[1,8,32,1024]{3,2,1,0:T(8,128)(2,1)S(1)}, u32[]{:S(2)}, u32[]{:S(2)}) collective-permute-start(bf16[1,8,32,1024]{3,2,1,0:T(8,128)(2,1)S(1)} %fusion.11), channel_id=1, source_target_pairs={{0,28},{4,0},{8,4},{12,8},{16,12},{20,16},{24,20},{28,24},{1,29},{... | collective-permute-start | bytes 1572872 | tf_op jit(solution)/shard_map/ppermute | solution.py:19
  62.7 20.0 %copy-start.17 = (s32[4096]{0:T(1024)}, s32[4096]{0:T(1024)S(1)}, u32[]{:S(2)}) copy-start(s32[4096]{0:T(1024)S(1)} %eq.39) | copy-start | bytes 49156
  82.7 4.0 collective-permute-start.1
  86.2 1.5 collective-permute-start.3
  88.1 19.4 %copy-start.5 = (bf16[1,4,8,8,1024]{4,3,2,1,0:T(8,128)(2,1)}, bf16[1,4,8,8,1024]{4,3,2,1,0:T(8,128)(2,1)S(1)}, u32[]{:S(2)}) copy-start(bf16[1,4,8,8,1024]{4,3,2,1,0:T(8,128)(2,1)S(1)} %copy.169) | copy-start | bytes 1572868
  110.2 34.6 %copy-start.13 = (bf16[256,1024]{1,0:T(8,128)(2,1)S(1)}, bf16[256,1024]{1,0:T(8,128)(2,1)}, u32[]{:S(2)}) copy-start(bf16[256,1024]{1,0:T(8,128)(2,1)} %multiply_convert_fusion.3) | copy-start | bytes 1572868
  181.2 1.6 collective-permute-start.4
  183.0 17.0 %collective-permute-start.5 = (bf16[1,8,32,1024]{3,2,1,0:T(8,128)(2,1)S(1)}, bf16[1,8,32,1024]{3,2,1,0:T(8,128)(2,1)}, u32[]{:S(2)}, u32[]{:S(2)}) collective-permute-start(bf16[1,8,32,1024]{3,2,1,0:T(8,128)(2,1)S(1)} %fusion.25), channel_id=1, source_target_pairs={{0,4},{4,8},{8,12},{12,16},{16,20},{20,24},{24,28},{28,0},{1,5},{5... | collective-permute-start | bytes 1572872 | tf_op jit(solution)/shard_map/ppermute | solution.py:19
  191.9 10.3 %copy-start.6 = (bf16[1,4,8,8,1024]{4,3,2,1,0:T(8,128)(2,1)S(1)}, bf16[1,4,8,8,1024]{4,3,2,1,0:T(8,128)(2,1)}, u32[]{:S(2)}) copy-start(bf16[1,4,8,8,1024]{4,3,2,1,0:T(8,128)(2,1)} %copy-done.5) | copy-start | bytes 1572868
  202.1 145.0 %reduce-scatter.3.cloned.1.call-start = ((), (), s32[]{:S(2)}) async-start(), calls=%async_computation.4 | async-start | bytes 3538944 | tf_op jit(solution)/shard_map/reduce_scatter | solution.py:227
  204.4 142.8 %copy-start.7 = (f32[12,64,64]{1,2,0:T(8,128)S(1)}, f32[12,64,64]{1,2,0:T(8,128)}, u32[]{:S(2)}) copy-start(f32[12,64,64]{1,2,0:T(8,128)} %get-tuple-element.84) | copy-start | bytes 589828
  204.4 143.1 %copy-start.18 = (s32[4096]{0:T(1024)S(1)}, s32[4096]{0:T(1024)}, u32[]{:S(2)}) copy-start(s32[4096]{0:T(1024)} %copy-done.17) | copy-start | bytes 49156
  204.4 193.2 %all-reduce.9.cloned.1.call-start = ((), (), s32[]{:S(2)}) async-start(), calls=%async_computation.8 | async-start | bytes 393216 | tf_op jit(solution)/shard_map/psum | solution.py:13
  270.3 134.1 %reduce-scatter.5.cloned.1.call-start = ((), (), s32[]{:S(2)}) async-start(), calls=%async_computation.5 | async-start | bytes 491520 | tf_op jit(solution)/shard_map/reduce_scatter | solution.py:235
  (11 other events, 46.8 us)
Sparse Core Ops, SparseCore 0:
  10.1 43.0 all-gather.3
  55.3 52.0 all-gather.7
  109.0 35.7 all-gather.5
  202.2 67.9 all-reduce.6
  273.7 73.3 reduce-scatter.2
  349.3 31.1 all-reduce.8
  383.5 20.8 reduce-scatter.4
